TPU v7x, 32 devices: a whole 2x2x4 slice. The times are simulated.
32 devices in a mesh: groups: 2 (over y), fsdp: 4 (over z), expert: 4 (over x, core).
Axes of the slice: x: 2, y: 2, z: 4, core: 2. Of those that a mesh axis runs over, the one named last changes fastest.
Arguments:
- queries: bfloat16 [512, 2048], P(('groups', 'fsdp'), 'expert'), parts along dimension 0, may hold values from -14 to 14
- keys: bfloat16 [8, 2048, 512], P(('groups', 'fsdp'), None, 'expert'), parts along dimension 0, may hold values from -14 to 14
- values: bfloat16 [8, 2048, 512], P(('groups', 'fsdp'), None, 'expert'), parts along dimension 0, may hold values from -4 to 4
- out_weight: bfloat16 [2048, 4096], P('expert', 'fsdp'), may hold values from -0.5 to 0.5
- residual: bfloat16 [512, 4096], P(('groups', 'fsdp')), parts along dimension 0, may hold values from -3 to 3
- norm_gain: float32 [4096], replicated, may hold values from 0.5 to 1.5
- route_ids: int32 [512, 2], P(('groups', 'fsdp')), parts along dimension 0, may hold values from 0 to 7, as said below
- route_slots: int32 [512, 2], P(('groups', 'fsdp')), parts along dimension 0, may hold values from 0 to 23, as said below
- route_weights: int32 [512, 2], P(('groups', 'fsdp')), parts along dimension 0, may hold values from 1 to 65535, as said below
- w_gate: bfloat16 [8, 4096, 7168], P('expert', None, 'fsdp'), may hold values from -0.09375 to 0.09375
- w_up: bfloat16 [8, 4096, 7168], P('expert', None, 'fsdp'), may hold values from -0.09375 to 0.09375
- w_down: bfloat16 [8, 7168, 4096], P('expert', 'fsdp'), may hold values from -0.0625 to 0.0625
Outputs:
- layer_out: bfloat16 [512, 4096], P(('groups', 'fsdp'), 'expert'), parts along dimension 0
There are 2 independent parts, one for each index of `groups`. A program takes and returns all parts, laid end to end along the dimension named above; an argument that names none is the same for every part. Nothing has to cross between parts.
Inputs may be any that keep to these rules, and one draw needn't show every extreme that they name: `route_ids`: each row names two different experts. Among the rows of one block, no expert is named more than 24 times and no group of experts 2 g and 2 g + 1 more than 36 times; one expert, the same for all blocks, is named exactly 24 times in every block and its group exactly 36 times; every expert is named in every block. `route_slots`: within one block, the routes to one expert hold the slots 0 to their count - 1, each once. `route_weights`: the two entries of a row sum to 65536.
All inputs are finite; a program needn't handle non-finite values.
Results may differ from a plain program's by a relative error of at most 0.02.
Values may be sent and summed in bfloat16 or wider, within the bound.
No kernel may reach another device: no remote copies, remote signals or barrier semaphores. Data moves between devices by JAX's collectives and lax.ppermute only.
A program may use at most 192 MiB of HBM per device.

v0:
```python
import jax
import jax.numpy as jnp
from jax import lax
from jax.sharding import PartitionSpec as P

HEAD_DIM = 128
GCAP = 36
eps = 1e-05


def attend(queries, keys, values):
    block = queries.shape[0]
    context = keys.shape[1]
    kv_dev = keys.shape[2] // HEAD_DIM
    heads_dev = queries.shape[1] // HEAD_DIM
    group = heads_dev // kv_dev
    query_heads = queries.reshape(block, kv_dev, group, HEAD_DIM)
    key_heads = keys[0].reshape(context, kv_dev, HEAD_DIM)
    value_heads = values[0].reshape(context, kv_dev, HEAD_DIM)
    scores = jnp.einsum(
        "qcgd,kcd->cgqk", query_heads, key_heads, preferred_element_type=jnp.float32
    ) * HEAD_DIM ** (-0.5)
    key_pos = jnp.arange(context)
    query_pos = context - block + jnp.arange(block)
    allowed = key_pos[None, :] <= query_pos[:, None]
    masked = jnp.where(allowed, scores, -1e30)
    highest = jnp.max(masked, axis=-1, keepdims=True)
    weights = jnp.where(allowed, jnp.exp(masked - highest), 0.0)
    probs = (weights / jnp.sum(weights, axis=-1, keepdims=True)).astype(jnp.bfloat16)
    heads_out = jnp.einsum("cgqk,kcd->qcgd", probs, value_heads, preferred_element_type=jnp.float32)
    return heads_out.astype(jnp.bfloat16).reshape(block, heads_dev * HEAD_DIM)


def per_device(
    queries,
    keys,
    values,
    out_weight,
    residual,
    norm_gain,
    route_ids,
    route_slots,
    route_weights,
    w_gate,
    w_up,
    w_down,
):
    heads_out = attend(queries, keys, values)
    partial_attn = jnp.dot(
        heads_out,
        lax.all_gather(out_weight, "fsdp", axis=1, tiled=True),
        preferred_element_type=jnp.float32,
    )
    attn = lax.psum(partial_attn.astype(jnp.bfloat16), "expert").astype(jnp.float32)
    hstate = (residual.astype(jnp.float32) + attn).astype(jnp.bfloat16)
    state = hstate.astype(jnp.float32)
    scale = lax.rsqrt(jnp.mean(state * state, axis=-1, keepdims=True) + eps)
    normed = (state * scale * norm_gain).astype(jnp.bfloat16)
    group_index = lax.axis_index("expert")
    first_expert = 2 * group_index
    within = route_ids - first_expert
    in_group = (within >= 0) & (within < 2)
    lead_count = jnp.sum((route_ids == first_expert).astype(jnp.int32))
    target = jnp.where(in_group, route_slots + within * lead_count, -1)
    row_ids = jnp.arange(GCAP)
    one_hot = (
        (target[None, :, 0] == row_ids[:, None]) | (target[None, :, 1] == row_ids[:, None])
    ).astype(jnp.bfloat16)
    dispatch = jnp.dot(one_hot, normed, preferred_element_type=jnp.float32).astype(jnp.bfloat16)
    second = (row_ids >= lead_count).astype(jnp.bfloat16)
    rows = lax.all_gather(dispatch, "fsdp", axis=0, tiled=True)
    labels = lax.all_gather(second, "fsdp", axis=0, tiled=True)
    gate = jnp.einsum("nd,edf->enf", rows, w_gate, preferred_element_type=jnp.float32)
    upper = jnp.einsum("nd,edf->enf", rows, w_up, preferred_element_type=jnp.float32)
    labels_f = labels.astype(jnp.float32)
    keep = jnp.stack([1.0 - labels_f, labels_f], axis=0)[:, :, None]
    values_new = (jax.nn.silu(gate) * upper * keep).astype(jnp.bfloat16)
    flat_out = lax.psum_scatter(
        jnp.einsum("enf,efd->nd", values_new, w_down, preferred_element_type=jnp.float32).astype(
            jnp.bfloat16
        ),
        "fsdp",
        scatter_dimension=0,
        tiled=True,
    ).astype(jnp.float32)
    row_index = route_slots + within * lead_count
    safe_index = jnp.where(in_group, row_index, 0)
    shares = jnp.where(in_group, route_weights.astype(jnp.float32) / 65536.0, 0.0)
    picked = jnp.take(flat_out, safe_index, axis=0)
    contrib = jnp.sum(shares[:, :, None] * picked, axis=1)
    moe = lax.psum_scatter(
        contrib.astype(jnp.bfloat16), "expert", scatter_dimension=1, tiled=True
    ).astype(jnp.float32)
    width = moe.shape[1]
    own_state = lax.dynamic_slice_in_dim(hstate, group_index * width, width, 1)
    return (own_state.astype(jnp.float32) + moe).astype(jnp.bfloat16)


def solution(mesh):
    in_specs = (
        P(("groups", "fsdp"), "expert"),
        P(("groups", "fsdp"), None, "expert"),
        P(("groups", "fsdp"), None, "expert"),
        P("expert", "fsdp"),
        P(("groups", "fsdp"), None),
        P(),
        P(("groups", "fsdp"), None),
        P(("groups", "fsdp"), None),
        P(("groups", "fsdp"), None),
        P("expert", None, "fsdp"),
        P("expert", None, "fsdp"),
        P("expert", "fsdp", None),
    )
    out_specs = P(("groups", "fsdp"), "expert")
    return jax.shard_map(
        per_device, mesh=mesh, in_specs=in_specs, out_specs=out_specs, check_vma=False
    )
```

profile of v0, /device:TPU:0, one launch (start us, length us, event | category | flops | bytes accessed | tf_op | source)
XLA Modules:
  0.0 273.5 jit_solution(8926764271031604778)
XLA Ops:
  6.5 0.0 copy-start
  6.5 0.0 all-gather.4.cloned.1.call-start
  6.5 0.7 all-gather.4.cloned.1.call-update
  7.3 0.0 all-reduce.5.cloned.1.call-start
  7.3 0.1 iota_compare_fusion
  7.5 0.1 copy-done
  7.6 1.5 fusion.39
  9.1 0.5 fusion.13
  9.6 0.0 copy-done.8
  9.6 0.7 fusion.14
  10.3 0.1 copy.23
  10.4 0.6 fusion.35
  11.1 81.3 %all-gather.4.cloned.1.call-done = bf16[512,4096]{1,0:T(8,128)(2,1)} async-done(((bf16[512,1024]{1,0:T(8,128)(2,1)}), bf16[512,4096]{1,0:T(8,128)(2,1)}) %all-gather.4.cloned.1.call-update) | async-done | bytes 4194320 | tf_op jit(solution)/shard_map/all_gather | solution.py:51
  92.4 3.9 %convolution_convert_fusion = bf16[64,4096]{1,0:T(8,128)(2,1)} fusion(bf16[512,4096]{1,0:T(8,128)(2,1)} %all-gather.4.cloned.1.call-done, bf16[8,8,4,128]{3,2,1,0:T(4,128)(2,1)S(1)} %bitcast.74), kind=kOutput, calls=%fused_computation.3 | convolution fusion | flops 268697600 | bytes 4784128 | tf_op jit(solution)/shard_map/dot_general | solution.py:49
  96.3 0.0 all-reduce.5.cloned.1.call-update
  96.3 0.0 all-gather.6.cloned.1.call-start
  96.4 0.7 broadcast_select_fusion
  97.0 31.3 %all-reduce.5.cloned.1.call-done = bf16[64,4096]{1,0:T(8,128)(2,1)} async-done(((bf16[64,4096]{1,0:T(8,128)(2,1)}), bf16[64,4096]{1,0:T(8,128)(2,1)}) %all-reduce.5.cloned.1.call-update) | async-done | bytes 524304 | tf_op jit(solution)/shard_map/psum | solution.py:54
  128.4 1.3 fusion.15
  129.7 1.1 fusion.2
  130.8 0.0 all-gather.6.cloned.1.call-update
  130.8 0.0 reduce-scatter.4.cloned.1.call-start
  130.9 0.7 fusion.38
  132.2 0.7 compare_convert_fusion
  132.8 0.2 dynamic-update-slice
  133.1 11.8 %all-reduce = bf16[144]{0:T(256)(128)(2,1)S(1)} all-reduce(bf16[144]{0:T(256)(128)(2,1)S(1)} %dynamic-update-slice), channel_id=1, replica_groups=mesh['groups'=2,'fsdp'=4,'expert'=4] {'fsdp'}, use_global_device_ids=true, to_apply=%add | all-reduce | flops 144 | bytes 576
  144.9 0.7 compare_and_fusion
  145.5 0.1 copy.26
  145.6 0.1 reshape.63
  145.8 0.1 copy.25
  145.9 0.1 copy.24
  146.7 17.0 %all-gather.6.cloned.1.call-done = bf16[4,36,4096]{2,1,0:T(8,128)(2,1)} async-done(((bf16[1,36,4096]{2,1,0:T(8,128)(2,1)}), bf16[4,36,4096]{2,1,0:T(8,128)(2,1)}) %all-gather.6.cloned.1.call-update) | async-done | bytes 1179664 | tf_op jit(solution)/shard_map/all_gather | solution.py:71
  163.6 2.2 reshape.80
  165.9 12.0 %convolution_bitcast_fusion.2 = f32[2,144,1792]{2,1,0:T(8,128)S(1)} fusion(bf16[144,4096,1]{1,0,2:T(8,128)(2,1)} %reshape.80, bf16[2,4096,1792]{2,1,0:T(8,128)(2,1)} %param.21), kind=kOutput, calls=%fused_computation.7 | convolution fusion | flops 4227858432 | bytes 32604160 | tf_op jit(solution)/shard_map/nd,edf->enf/dot_general | solution.py:73
  177.9 0.0 copy-done.2
  177.9 22.2 %fusion.1 = bf16[144,4096]{1,0:T(8,128)(2,1)} fusion(bf16[2,1792,4096]{2,1,0:T(8,128)(2,1)} %param.23, bf16[144,4096,1]{1,0,2:T(8,128)(2,1)} %reshape.80, bf16[2,4096,1792]{2,1,0:T(8,128)(2,1)} %param.22, f32[2,144,1792]{2,1,0:T(8,128)S(1)} %convolution_bitcast_fusion.2, f32[2,144]{1,0:T(2,128)S(1)} %pad_maximum_fusion), kind=kOutput, calls=%fused_computation.2 | convolution fusion | flops 8459919360 | bytes 63145088 | tf_op jit(solution)/shard_map/enf,efd->nd/dot_general | solution.py:79
  200.1 29.1 %fusion = bf16[40,4096]{1,0:T(8,128)(2,1)S(1)} fusion(bf16[144,4096]{1,0:T(8,128)(2,1)} %fusion.1), kind=kCustom, calls=%all-reduce-scatter | all-reduce-scatter fusion | flops 655361 | bytes 1507840
  229.2 1.8 collective-permute-start
  231.0 2.3 collective-permute-done
  233.3 0.4 concatenate
  233.7 0.1 dynamic-slice_convert_fusion
  233.8 1.3 gather_fusion
  235.1 0.0 copy-start.1
  235.2 2.3 reshape.62
  237.4 6.0 %multiply_reduce_fusion = bf16[64,4096]{1,0:T(8,128)(2,1)} fusion(f32[64,2,4096]{2,1,0:T(2,128)} %reshape.62, pred[64,2]{1,0:T(8,128)(4,1)S(1)} %copy.25, f32[64,2]{1,0:T(8,128)S(1)} %copy.24), kind=kLoop, calls=%fused_computation.14 | loop fusion | flops 1310720 | bytes 2622080 | tf_op jit(solution)/shard_map/reduce_sum | solution.py:90
  243.5 0.0 reduce-scatter.4.cloned.1.call-update
  243.5 21.9 %reduce-scatter.4.cloned.1.call-done = bf16[64,1024]{1,0:T(8,128)(2,1)} async-done(((bf16[64,4096]{1,0:T(8,128)(2,1)}), bf16[64,1024]{1,0:T(8,128)(2,1)}) %reduce-scatter.4.cloned.1.call-update) | async-done | bytes 131088 | tf_op jit(solution)/shard_map/reduce_scatter | solution.py:91
  265.4 1.7 add_convert_fusion.1
  (25 shorter events, 0.1 us)
Async XLA Ops:
  6.5 1.0 copy-start
  6.5 85.9 %all-gather.4.cloned.1.call-start = ((), (), s32[]{:S(2)}) async-start(), calls=%async_computation.1 | async-start | bytes 5242880 | tf_op jit(solution)/shard_map/all_gather | solution.py:51
  7.3 121.1 %all-reduce.5.cloned.1.call-start = ((), (), s32[]{:S(2)}) async-start(), calls=%async_computation.2 | async-start | bytes 1048576 | tf_op jit(solution)/shard_map/psum | solution.py:54
  7.6 2.0 copy-start.8
  9.6 0.8 copy-start.4
  9.6 1.5 copy-start.7
  92.4 4.0 %copy-start.5 = (s32[64,2]{0,1:T(2,128)S(1)}, s32[64,2]{0,1:T(2,128)}, u32[]{:S(2)}) copy-start(s32[64,2]{0,1:T(2,128)} %param.19) | copy-start | bytes 1540
  92.4 36.0 %copy-start.3 = (bf16[64,4096]{1,0:T(8,128)(2,1)S(1)}, bf16[64,4096]{1,0:T(8,128)(2,1)}, u32[]{:S(2)}) copy-start(bf16[64,4096]{1,0:T(8,128)(2,1)} %param.16) | copy-start | bytes 1572868
  96.3 33.4 %copy-start.9 = (f32[4096]{0:T(1024)S(1)}, f32[4096]{0:T(1024)}, u32[]{:S(2)}) copy-start(f32[4096]{0:T(1024)} %param.17) | copy-start | bytes 49156
  96.3 34.6 %copy-start.6 = (u32[32]{0:T(128)S(1)}, u32[32]{0:T(128)}, u32[]{:S(2)}) copy-start(u32[32]{0:T(128)} %constant.60) | copy-start | bytes 388
  96.3 67.3 %all-gather.6.cloned.1.call-start = ((), (), s32[]{:S(2)}) async-start(), calls=%async_computation.4 | async-start | bytes 1638400 | tf_op jit(solution)/shard_map/all_gather | solution.py:71
  129.7 48.2 %copy-start.2 = (bf16[64,4096]{1,0:T(8,128)(2,1)}, bf16[64,4096]{1,0:T(8,128)(2,1)S(1)}, u32[]{:S(2)}) copy-start(bf16[64,4096]{1,0:T(8,128)(2,1)S(1)} %get-tuple-element.10) | copy-start | bytes 1572868
  130.8 134.5 %reduce-scatter.4.cloned.1.call-start = ((), (), s32[]{:S(2)}) async-start(), calls=%async_computation.3 | async-start | bytes 655360 | tf_op jit(solution)/shard_map/reduce_scatter | solution.py:91
  229.2 4.1 %collective-permute-start = (bf16[12,4096]{1,0:T(8,128)(2,1)S(1)}, bf16[12,4096]{1,0:T(8,128)(2,1)S(1)}, u32[]{:S(2)}, u32[]{:S(2)}) collective-permute-start(bf16[12,4096]{1,0:T(8,128)(2,1)S(1)} %slice.10), channel_id=1, source_target_pairs={{0,4},{4,8},{8,12},{1,5},{5,9},{9,13},{2,6},{6,10},{10,14},{3,7},{... | collective-permute-start | bytes 294920
  235.1 31.9 %copy-start.1 = (bf16[1,2048,128]{2,1,0:T(8,128)(2,1)S(1)}, bf16[1,2048,128]{2,1,0:T(8,128)(2,1)}, u32[]{:S(2)}) copy-start(bf16[1,2048,128]{2,1,0:T(8,128)(2,1)} %param.13) | copy-start | bytes 1572868
Sparse Core Ops, SparseCore 0:
  8.9 83.4 all-gather.3
  96.4 31.8 all-reduce.4
  130.9 32.6 all-gather.5
  243.6 21.6 reduce-scatter.3
where the time goes:
time: 274 us
  waiting for transfers between devices  155 us (57%)
  matrix products  41.3 us (15%)
  blocking collectives  40.8 us (15%)
  between operations  14.7 us (5%)
  other arithmetic  12.4 us (5%)
  local copies, waits for them, and re-layouts  7.87 us (3%)
    all_gather x1, waiting for transfers between devices, per_device(): lax.all_gather(out_weight, 'fsdp', axis=1, tiled=True)  81.3 us
    unnamed x2, blocking collectives  40.8 us
    psum x1, waiting for transfers between devices, per_device(): lax.psum(partial_attn.astype(jnp.bfloat16), 'expert').astype(jnp.float32)  31.3 us
    dot_general x1, matrix products, per_device(): jnp.einsum('enf,efd->nd', values_new, w_down, preferred_element_type=jnp....  22.2 us
    reduce_scatter x1, waiting for transfers between devices, per_device(): lax.psum_scatter(contrib.astype(jnp.bfloat16), 'expert', scatter_dimensio...  21.9 us
    all_gather x1, waiting for transfers between devices, per_device(): rows = lax.all_gather(dispatch, 'fsdp', axis=0, tiled=True)  17 us
    dot_general x1, matrix products, per_device(): jnp.einsum('nd,edf->enf', rows, w_gate, preferred_element_type=jnp.float32)  12 us
    reduce_sum x1, other arithmetic, per_device(): contrib = jnp.sum(shares[:, :, None] * picked, axis=1)  6.02 us
  transfers between devices with their start and end apart: 5, of which 5 were waited for; matrix products, arithmetic and copies ran while one was open for 3% of the time, Pallas kernels for 0%

commit v1 on v0

--- a/solution.py
+++ b/solution.py
@@ -6,6 +6,11 @@
 HEAD_DIM = 128
 GCAP = 36
 eps = 1e-05
+
+
+def all_by_exchange(x, mesh_axis, along):
+    sent = jnp.stack([x] * lax.axis_size(mesh_axis))
+    return jnp.concatenate(lax.all_to_all(sent, mesh_axis, 0, 0), axis=along)
 
 
 def attend(queries, keys, values):
@@ -68,7 +73,7 @@
     ).astype(jnp.bfloat16)
     dispatch = jnp.dot(one_hot, normed, preferred_element_type=jnp.float32).astype(jnp.bfloat16)
     second = (row_ids >= lead_count).astype(jnp.bfloat16)
-    rows = lax.all_gather(dispatch, "fsdp", axis=0, tiled=True)
+    rows = all_by_exchange(dispatch, "fsdp", 0)
     labels = lax.all_gather(second, "fsdp", axis=0, tiled=True)
     gate = jnp.einsum("nd,edf->enf", rows, w_gate, preferred_element_type=jnp.float32)
     upper = jnp.einsum("nd,edf->enf", rows, w_up, preferred_element_type=jnp.float32)

time: 274 us -> 278 us (1.015)
  waiting for transfers between devices: 155 us -> 140 us
  blocking collectives: 40.8 us -> 55.5 us
  starting transfers between devices: 1.9 us -> 6.38 us
    all_gather x1 -> x0, waiting for transfers between devices: 17 us -> none  [per_device(): rows = lax.all_gather(dispatch, 'fsdp', axis=0, tiled=True)]
    unnamed x2, blocking collectives: 40.8 us -> 55.5 us
    all_to_all x0 -> x1, starting transfers between devices: none -> 4.6 us  [all_by_exchange(): return jnp.concatenate(lax.all_to_all(sent, mesh_axis, 0, 0), axis=along)]
  transfers between devices with their start and end apart: 5 -> 5, of which waited for: 5 -> 5; matrix products, arithmetic and copies ran while one was open for 3% -> 2% of each run, Pallas kernels for 0% -> 0%
where the time goes in v1:
time: 278 us
  waiting for transfers between devices  140 us (50%)
  blocking collectives  55.5 us (20%)
  matrix products  40.6 us (15%)
  between operations  14.6 us (5%)
  other arithmetic  12.4 us (4%)
  local copies, waits for them, and re-layouts  7.97 us (3%)
  starting transfers between devices  6.38 us (2%)
    all_gather x1, waiting for transfers between devices, per_device(): lax.all_gather(out_weight, 'fsdp', axis=1, tiled=True)  81.3 us
    unnamed x2, blocking collectives  55.5 us
    psum x1, waiting for transfers between devices, per_device(): lax.psum(partial_attn.astype(jnp.bfloat16), 'expert').astype(jnp.float32)  31.4 us
    dot_general x1, matrix products, per_device(): jnp.einsum('enf,efd->nd', values_new, w_down, preferred_element_type=jnp....  22.2 us
    reduce_scatter x1, waiting for transfers between devices, per_device(): lax.psum_scatter(contrib.astype(jnp.bfloat16), 'expert', scatter_dimensio...  22.1 us
    dot_general x1, matrix products, per_device(): jnp.einsum('nd,edf->enf', rows, w_gate, preferred_element_type=jnp.float32)  12 us
    reduce_sum x1, other arithmetic, per_device(): contrib = jnp.sum(shares[:, :, None] * picked, axis=1)  6.02 us
  transfers between devices with their start and end apart: 5, of which 5 were waited for; matrix products, arithmetic and copies ran while one was open for 2% of the time, Pallas kernels for 0%

profile of v1, /device:TPU:0, one launch (start us, length us, event | category | flops | bytes accessed | tf_op | source)
XLA Modules:
  0.0 277.6 jit_solution(9931149364218960135)
XLA Ops:
  6.5 0.0 copy-start
  6.5 0.0 all-gather.2.cloned.1.call-start
  6.5 0.7 all-gather.2.cloned.1.call-update
  7.3 0.0 all-reduce.5.cloned.1.call-start
  7.3 0.1 iota_compare_fusion
  7.5 0.1 copy-done
  7.6 1.5 fusion.38
  9.1 0.5 fusion.12
  9.6 0.7 fusion.13
  10.3 0.1 copy.23
  10.4 0.6 fusion.34
  11.1 81.3 %all-gather.2.cloned.1.call-done = bf16[512,4096]{1,0:T(8,128)(2,1)} async-done(((bf16[512,1024]{1,0:T(8,128)(2,1)}), bf16[512,4096]{1,0:T(8,128)(2,1)}) %all-gather.2.cloned.1.call-update) | async-done | bytes 4194320 | tf_op jit(solution)/shard_map/all_gather | solution.py:56
  92.4 3.9 %convolution_convert_fusion = bf16[64,4096]{1,0:T(8,128)(2,1)} fusion(bf16[512,4096]{1,0:T(8,128)(2,1)} %all-gather.2.cloned.1.call-done, bf16[8,8,4,128]{3,2,1,0:T(4,128)(2,1)S(1)} %bitcast.72), kind=kOutput, calls=%fused_computation.3 | convolution fusion | flops 268697600 | bytes 4784128 | tf_op jit(solution)/shard_map/dot_general | solution.py:54
  96.3 0.0 all-reduce.5.cloned.1.call-update
  96.3 0.7 broadcast_select_fusion
  97.0 31.4 %all-reduce.5.cloned.1.call-done = bf16[64,4096]{1,0:T(8,128)(2,1)} async-done(((bf16[64,4096]{1,0:T(8,128)(2,1)}), bf16[64,4096]{1,0:T(8,128)(2,1)}) %all-reduce.5.cloned.1.call-update) | async-done | bytes 524304 | tf_op jit(solution)/shard_map/psum | solution.py:59
  128.4 0.0 copy-done.3
  128.4 1.3 fusion.14
  129.7 0.3 convolution_convert_fusion.1
  130.1 0.0 copy-start.6
  130.1 1.2 stack.16
  131.3 4.6 %all-to-all-start = ((bf16[4,36,4096]{2,1,0:T(8,128)(2,1)}), bf16[4,36,4096]{2,1,0:T(8,128)(2,1)S(1)}, u32[]{:S(2)}, u32[]{:S(2)}) async-start(bf16[4,36,4096]{2,1,0:T(8,128)(2,1)} %stack.16), calls=%async_computation | async-start | bytes 2621440 | tf_op jit(solution)/shard_map/all_to_all | solution.py:13
  135.9 0.0 reduce-scatter.4.cloned.1.call-start
  135.9 0.7 fusion.37
  137.1 0.7 compare_convert_fusion
  137.8 0.2 dynamic-update-slice
  138.0 24.3 %all-reduce = bf16[144]{0:T(256)(128)(2,1)S(1)} all-reduce(bf16[144]{0:T(256)(128)(2,1)S(1)} %dynamic-update-slice), channel_id=1, replica_groups=mesh['groups'=2,'fsdp'=4,'expert'=4] {'fsdp'}, use_global_device_ids=true, to_apply=%add | all-reduce | flops 144 | bytes 576
  162.4 0.7 compare_and_fusion
  163.0 0.1 copy.26
  163.1 0.1 reshape.69
  163.3 0.1 copy.25
  163.4 0.1 copy.24
  164.2 2.3 all-to-all-done
  166.5 1.1 reshape.84
  167.6 12.0 %convolution_bitcast_fusion.2 = f32[2,144,1792]{2,1,0:T(8,128)S(1)} fusion(bf16[144,4096,1]{1,0,2:T(8,128)(2,1)} %reshape.84, bf16[2,4096,1792]{2,1,0:T(8,128)(2,1)} %param.21), kind=kOutput, calls=%fused_computation.6 | convolution fusion | flops 4227858432 | bytes 32604160 | tf_op jit(solution)/shard_map/nd,edf->enf/dot_general | solution.py:78
  179.7 22.2 %fusion.1 = bf16[144,4096]{1,0:T(8,128)(2,1)} fusion(bf16[2,1792,4096]{2,1,0:T(8,128)(2,1)} %param.23, bf16[144,4096,1]{1,0,2:T(8,128)(2,1)} %reshape.84, bf16[2,4096,1792]{2,1,0:T(8,128)(2,1)} %param.22, f32[2,144,1792]{2,1,0:T(8,128)S(1)} %convolution_bitcast_fusion.2, f32[2,144]{1,0:T(2,128)S(1)} %pad_maximum_fusion), kind=kOutput, calls=%fused_computation.2 | convolution fusion | flops 8459919360 | bytes 63145088 | tf_op jit(solution)/shard_map/enf,efd->nd/dot_general | solution.py:84
  201.9 31.1 %fusion = bf16[40,4096]{1,0:T(8,128)(2,1)S(1)} fusion(bf16[144,4096]{1,0:T(8,128)(2,1)} %fusion.1), kind=kCustom, calls=%all-reduce-scatter | all-reduce-scatter fusion | flops 655361 | bytes 1507840
  233.0 1.7 collective-permute-start
  234.8 2.3 collective-permute-done
  237.1 0.4 concatenate
  237.5 0.1 dynamic-slice_convert_fusion
  237.6 1.3 gather_fusion
  238.9 0.0 copy-start.1
  239.0 2.3 reshape.68
  241.2 6.0 %multiply_reduce_fusion = bf16[64,4096]{1,0:T(8,128)(2,1)} fusion(f32[64,2,4096]{2,1,0:T(2,128)} %reshape.68, pred[64,2]{1,0:T(8,128)(4,1)S(1)} %copy.25, f32[64,2]{1,0:T(8,128)S(1)} %copy.24), kind=kLoop, calls=%fused_computation.13 | loop fusion | flops 1310720 | bytes 2622080 | tf_op jit(solution)/shard_map/reduce_sum | solution.py:95
  247.3 0.0 reduce-scatter.4.cloned.1.call-update
  247.3 22.1 %reduce-scatter.4.cloned.1.call-done = bf16[64,1024]{1,0:T(8,128)(2,1)} async-done(((bf16[64,4096]{1,0:T(8,128)(2,1)}), bf16[64,1024]{1,0:T(8,128)(2,1)}) %reduce-scatter.4.cloned.1.call-update) | async-done | bytes 131088 | tf_op jit(solution)/shard_map/reduce_scatter | solution.py:96
  269.4 1.7 add_convert_fusion.1
  (25 shorter events, 0.1 us)
Async XLA Ops:
  6.5 1.0 copy-start
  6.5 85.9 %all-gather.2.cloned.1.call-start = ((), (), s32[]{:S(2)}) async-start(), calls=%async_computation.2 | async-start | bytes 5242880 | tf_op jit(solution)/shard_map/all_gather | solution.py:56
  7.3 121.1 %all-reduce.5.cloned.1.call-start = ((), (), s32[]{:S(2)}) async-start(), calls=%async_computation.3 | async-start | bytes 1048576 | tf_op jit(solution)/shard_map/psum | solution.py:59
  7.6 2.0 copy-start.8
  9.6 0.8 copy-start.4
  9.6 1.5 copy-start.7
  92.4 3.9 %copy-start.5 = (s32[64,2]{0,1:T(2,128)S(1)}, s32[64,2]{0,1:T(2,128)}, u32[]{:S(2)}) copy-start(s32[64,2]{0,1:T(2,128)} %param.19) | copy-start | bytes 1540
  92.4 36.0 %copy-start.3 = (bf16[64,4096]{1,0:T(8,128)(2,1)S(1)}, bf16[64,4096]{1,0:T(8,128)(2,1)}, u32[]{:S(2)}) copy-start(bf16[64,4096]{1,0:T(8,128)(2,1)} %param.16) | copy-start | bytes 1572868
  96.3 33.4 %copy-start.9 = (f32[4096]{0:T(1024)S(1)}, f32[4096]{0:T(1024)}, u32[]{:S(2)}) copy-start(f32[4096]{0:T(1024)} %param.17) | copy-start | bytes 49156
  129.7 1.6 copy-start.2
  130.1 5.8 %copy-start.6 = (u32[32]{0:T(128)S(1)}, u32[32]{0:T(128)}, u32[]{:S(2)}) copy-start(u32[32]{0:T(128)} %constant.60) | copy-start | bytes 388
  131.3 35.2 %all-to-all-start = ((bf16[4,36,4096]{2,1,0:T(8,128)(2,1)}), bf16[4,36,4096]{2,1,0:T(8,128)(2,1)S(1)}, u32[]{:S(2)}, u32[]{:S(2)}) async-start(bf16[4,36,4096]{2,1,0:T(8,128)(2,1)} %stack.16), calls=%async_computation | async-start | bytes 2621440 | tf_op jit(solution)/shard_map/all_to_all | solution.py:13
  135.9 133.6 %reduce-scatter.4.cloned.1.call-start = ((), (), s32[]{:S(2)}) async-start(), calls=%async_computation.4 | async-start | bytes 655360 | tf_op jit(solution)/shard_map/reduce_scatter | solution.py:96
  233.0 4.1 %collective-permute-start = (bf16[12,4096]{1,0:T(8,128)(2,1)S(1)}, bf16[12,4096]{1,0:T(8,128)(2,1)S(1)}, u32[]{:S(2)}, u32[]{:S(2)}) collective-permute-start(bf16[12,4096]{1,0:T(8,128)(2,1)S(1)} %slice.10), channel_id=1, source_target_pairs={{0,4},{4,8},{8,12},{1,5},{5,9},{9,13},{2,6},{6,10},{10,14},{3,7},{... | collective-permute-start | bytes 294920
  238.9 32.2 %copy-start.1 = (bf16[1,2048,128]{2,1,0:T(8,128)(2,1)S(1)}, bf16[1,2048,128]{2,1,0:T(8,128)(2,1)}, u32[]{:S(2)}) copy-start(bf16[1,2048,128]{2,1,0:T(8,128)(2,1)} %param.13) | copy-start | bytes 1572868
Sparse Core Ops, SparseCore 0:
  8.9 83.4 all-gather.1
  96.4 31.8 all-reduce.4
  247.4 21.9 reduce-scatter.3
